TPU v7x, 256 devices: a whole 4x4x8 slice. The times are simulated.
256 devices in a mesh: row: 16 (over z, core), col: 16 (over x, y).
Axes of the slice: x: 4, y: 4, z: 8, core: 2. Of those that a mesh axis runs over, the one named last changes fastest.
Arguments:
- train_weight: bfloat16 [4, 4608, 8192], P(None, 'row', 'col')
- src_map: int32 [64], replicated, may hold values from 0 to 63, as said below
- tgt_map: int32 [64], replicated, may hold values from 0 to 63, as said below
- probe: bfloat16 [8192, 4608], P('row'), may hold values from -6 to 6
Outputs:
- codes: bfloat16 [4, 4608, 8192], P(None, None, 'col')
- peaks: float32 [4, 64], P(None, 'col')
- checked: bfloat16 [4, 8192, 8192], P(None, 'row', 'col')
Inputs may be any that keep to these rules, and one draw needn't show every extreme that they name: src_map is a permutation of 0 to 63. tgt_map is a permutation of 0 to 63. Call column k the slots k * 4 to (k + 1) * 4 - 1 of a map, and let C = 16. There are three different offsets a, b, c in 0 to C - 1, the same for every column, of which one is C / 2 and one is C - 1: the heads of training column k stand in serving columns (k - a) mod C (2 of them), (k - b) mod C (one) and (k - c) mod C (one).
All inputs are finite; a program needn't handle non-finite values. Where the computation divides by a largest or mean magnitude, that divisor is 1e-20 or more.
Results may differ from a plain program's by a relative error of at most 0.0049.
Values may be sent and summed in bfloat16 or wider, within the bound.
A program may use at most 128 MiB of HBM per device.

v0:
```python
import jax
import jax.numpy as jnp
from jax import lax
from jax.sharding import PartitionSpec as P

HDIM = 128


def passed_along(shard, axis, by):
    devices = lax.axis_size(axis)
    return lax.ppermute(shard, axis, [(i, (i + by) % devices) for i in range(devices)])


def per_device(train_weight, src_map, tgt_map, probe):
    col_count = lax.axis_size("col")
    heads_all = src_map.shape[0]
    per_col = heads_all // col_count
    layers = train_weight.shape[0]
    rows_here = train_weight.shape[1]
    column = lax.axis_index("col")
    slot_ids = jnp.arange(heads_all, dtype=jnp.int32)
    wanted = lax.dynamic_slice(tgt_map, (column * per_col,), (per_col,))
    local_four = train_weight.reshape(layers, rows_here, per_col, HDIM)
    target_pos = jnp.sum(
        (tgt_map[None, :] == src_map[:, None]).astype(jnp.int32) * slot_ids[None, :], axis=1
    )
    dest_col = target_pos // per_col
    own_col = slot_ids // per_col
    offset_all = (dest_col - own_col + col_count) % col_count
    sort_key = offset_all * per_col + slot_ids % per_col
    same_col = own_col[:, None] == own_col[None, :]
    before = sort_key[None, :] < sort_key[:, None]
    slot_rank = jnp.sum((same_col & before).astype(jnp.int32), axis=1)
    my_rank = lax.dynamic_slice(slot_rank, (column * per_col,), (per_col,))
    my_offset = lax.dynamic_slice(offset_all, (column * per_col,), (per_col,))
    local_ids = jnp.arange(per_col, dtype=jnp.int32)
    send_match = local_ids[:, None] == my_rank[None, :]
    buffer_offset = jnp.sum(send_match.astype(jnp.int32) * my_offset[None, :], axis=1)
    buffers = jnp.einsum(
        "ki,ldie->klde",
        send_match.astype(jnp.bfloat16),
        local_four,
        preferred_element_type=jnp.float32,
    ).astype(jnp.bfloat16)
    for bit in range((col_count - 1).bit_length()):
        stride = 1 << bit
        arrived = passed_along(buffers, "col", stride)
        taken = buffer_offset // stride % 2 == 1
        buffers = jnp.where(taken[:, None, None, None], arrived, buffers)
    source_slot = jnp.sum(
        (src_map[None, :] == wanted[:, None]).astype(jnp.int32) * slot_ids[None, :], axis=1
    )
    from_rank = jnp.take(slot_rank, source_slot)
    recv_sel = (from_rank[:, None] == local_ids[None, :]).astype(jnp.bfloat16)
    block_part = jnp.einsum(
        "klde,jk->ldje", buffers, recv_sel, preferred_element_type=jnp.float32
    ).astype(jnp.bfloat16)
    joined = lax.all_gather(
        block_part.reshape(layers, rows_here, per_col * HDIM), "row", axis=1, tiled=True
    )
    joined_four = joined.reshape(layers, -1, per_col, HDIM)
    peaks = jnp.max(jnp.abs(joined_four.astype(jnp.float32)), axis=(1, 3))
    codes = (joined_four.astype(jnp.float32) / (peaks[:, None, :, None] + 1e-06)).astype(
        jnp.bfloat16
    )
    codes = codes.reshape(layers, -1, per_col * HDIM)
    projected = jnp.einsum("td,lde->lte", probe, codes, preferred_element_type=jnp.float32)
    checked = (projected * jnp.repeat(peaks, HDIM, axis=1)[:, None, :]).astype(jnp.bfloat16)
    return (codes, peaks, checked)


def solution(mesh):
    in_specs = (P(None, "row", "col"), P(), P(), P("row", None))
    out_specs = (P(None, None, "col"), P(None, "col"), P(None, "row", "col"))
    return jax.shard_map(
        per_device, mesh=mesh, in_specs=in_specs, out_specs=out_specs, check_vma=False
    )
```

profile of v0, /device:TPU:1, one launch (start us, length us, event | category | flops | bytes accessed | tf_op | source)
XLA Modules:
  0.0 286.7 jit_solution(9566830135982782130)
XLA Ops:
  7.2 0.0 all-gather.2.cloned.1.call-start
  7.2 0.8 select_reduce_fusion
  8.1 2.5 reshape.254
  10.6 0.2 convert_reduce_fusion
  10.8 0.1 dynamic_slice.10
  10.9 0.8 convolution_convert_fusion.1
  11.7 2.2 collective-permute-start
  13.9 0.1 dynamic_slice.11
  13.9 0.1 select_reduce_fusion.1
  14.1 27.2 %collective-permute-done = bf16[4,4,288,128]{3,0,2,1:T(4,128)(2,1)S(1)} collective-permute-done((bf16[4,4,288,128]{3,0,2,1:T(4,128)(2,1)S(1)}, bf16[4,4,288,128]{3,0,2,1:T(4,128)(2,1)S(1)}, u32[]{:S(2)}, u32[]{:S(2)}) %collective-permute-start) | collective-permute-done | bytes 1179680 | tf_op jit(solution)/shard_map/ppermute | solution.py:11
  41.3 0.7 broadcast_select_fusion
  42.0 1.1 collective-permute-start.1
  43.1 27.0 %collective-permute-done.1 = bf16[4,4,288,128]{3,0,2,1:T(4,128)(2,1)S(1)} collective-permute-done((bf16[4,4,288,128]{3,0,2,1:T(4,128)(2,1)S(1)}, bf16[4,4,288,128]{3,0,2,1:T(4,128)(2,1)S(1)}, u32[]{:S(2)}, u32[]{:S(2)}) %collective-permute-start.1) | collective-permute-done | bytes 1179680 | tf_op jit(solution)/shard_map/ppermute | solution.py:11
  70.2 0.7 broadcast_select_fusion.1
  70.9 1.8 collective-permute-start.2
  72.7 23.7 %collective-permute-done.2 = bf16[4,4,288,128]{3,0,2,1:T(4,128)(2,1)S(1)} collective-permute-done((bf16[4,4,288,128]{3,0,2,1:T(4,128)(2,1)S(1)}, bf16[4,4,288,128]{3,0,2,1:T(4,128)(2,1)S(1)}, u32[]{:S(2)}, u32[]{:S(2)}) %collective-permute-start.2) | collective-permute-done | bytes 1179680 | tf_op jit(solution)/shard_map/ppermute | solution.py:11
  96.4 0.7 broadcast_select_fusion.2
  97.2 3.2 %collective-permute-start.3 = (bf16[4,4,288,128]{3,0,2,1:T(4,128)(2,1)S(1)}, bf16[4,4,288,128]{3,0,2,1:T(4,128)(2,1)S(1)}, u32[]{:S(2)}, u32[]{:S(2)}) collective-permute-start(bf16[4,4,288,128]{3,0,2,1:T(4,128)(2,1)S(1)} %broadcast_select_fusion.2), channel_id=1, source_target_pairs={{0,8},{1,9},{2,10},{3,11},{4,12},{5,13},{6,14},{7,15},{8,0},{9,1},... | collective-permute-start | bytes 3538952 | tf_op jit(solution)/shard_map/ppermute | solution.py:11
  100.3 0.1 dynamic_slice.9
  100.4 0.2 select_reduce_fusion.2
  100.6 0.6 gather_fusion
  101.3 21.2 %collective-permute-done.3 = bf16[4,4,288,128]{3,0,2,1:T(4,128)(2,1)S(1)} collective-permute-done((bf16[4,4,288,128]{3,0,2,1:T(4,128)(2,1)S(1)}, bf16[4,4,288,128]{3,0,2,1:T(4,128)(2,1)S(1)}, u32[]{:S(2)}, u32[]{:S(2)}) %collective-permute-start.3) | collective-permute-done | bytes 1179680 | tf_op jit(solution)/shard_map/ppermute | solution.py:11
  122.4 1.0 fusion.9
  123.4 1.3 reshape.255
  124.8 112.3 %all-gather.2.cloned.1.call-done = bf16[4,4608,512]{2,1,0:T(8,128)(2,1)} async-done(((bf16[4,288,512]{2,1,0:T(8,128)(2,1)}), bf16[4,4608,512]{2,1,0:T(8,128)(2,1)}) %all-gather.2.cloned.1.call-update) | async-done | bytes 18874384 | tf_op jit(solution)/shard_map/all_gather | solution.py:58
  237.0 7.4 %fusion = f32[4,512]{1,0:T(4,128)S(1)} fusion(bf16[4,4608,512]{2,1,0:T(8,128)(2,1)} %all-gather.2.cloned.1.call-done), kind=kLoop, calls=%fused_computation.3 | loop fusion | flops 28309504 | bytes 18882560 | tf_op jit(solution)/shard_map/reduce_max | solution.py:62
  244.4 0.1 reduce_max.18
  244.5 0.1 broadcast_bitcast_fusion
  244.6 0.1 broadcast_bitcast_fusion.1
  244.7 17.7 %fusion.1 = bf16[4,4608,512]{2,1,0:T(8,128)(2,1)} fusion(bf16[4,4608,512]{2,1,0:T(8,128)(2,1)} %all-gather.2.cloned.1.call-done, f32[4,512]{1,0:T(4,128)S(1)} %bitcast.37), kind=kLoop, calls=%fused_computation.4 | loop fusion | flops 28311552 | bytes 37756928 | tf_op jit(solution)/shard_map/convert_element_type | solution.py:63
  262.3 15.2 %fusion.6 = bf16[4,512,512]{1,2,0:T(8,128)(2,1)S(1)} fusion(f32[4,512]{1,0:T(4,128)S(1)} %bitcast.38, bf16[4,4608,512]{2,1,0:T(8,128)(2,1)} %fusion.1, bf16[512,4608]{1,0:T(8,128)(2,1)} %param.7), kind=kOutput, calls=%fused_computation.8 | convolution fusion | flops 9665773568 | bytes 25698304 | tf_op jit(solution)/shard_map/td,lde->lte/dot_general | solution.py:67
  277.5 2.4 copy.12
  (16 shorter events, 0.1 us)
Async XLA Ops:
  7.2 229.9 %all-gather.2.cloned.1.call-start = ((), (), s32[]{:S(2)}) async-start(), calls=%async_computation | async-start | bytes 20054016 | tf_op jit(solution)/shard_map/all_gather | solution.py:58
  11.7 29.7 %collective-permute-start = (bf16[4,4,288,128]{3,0,2,1:T(4,128)(2,1)S(1)}, bf16[4,4,288,128]{3,0,2,1:T(4,128)(2,1)S(1)}, u32[]{:S(2)}, u32[]{:S(2)}) collective-permute-start(bf16[4,4,288,128]{3,0,2,1:T(4,128)(2,1)S(1)} %convolution_convert_fusion.1), channel_id=1, source_target_pairs={{0,1},{1,2},{2,3},{3,4},{4,5},{5,6},{6,7},{7,8},{8,9},{9,10},{10,1... | collective-permute-start | bytes 3538952 | tf_op jit(solution)/shard_map/ppermute | solution.py:11
  42.0 28.1 %collective-permute-start.1 = (bf16[4,4,288,128]{3,0,2,1:T(4,128)(2,1)S(1)}, bf16[4,4,288,128]{3,0,2,1:T(4,128)(2,1)S(1)}, u32[]{:S(2)}, u32[]{:S(2)}) collective-permute-start(bf16[4,4,288,128]{3,0,2,1:T(4,128)(2,1)S(1)} %broadcast_select_fusion), channel_id=1, source_target_pairs={{0,2},{1,3},{2,4},{3,5},{4,6},{5,7},{6,8},{7,9},{8,10},{9,11},{10,... | collective-permute-start | bytes 3538952 | tf_op jit(solution)/shard_map/ppermute | solution.py:11
  70.9 25.6 %collective-permute-start.2 = (bf16[4,4,288,128]{3,0,2,1:T(4,128)(2,1)S(1)}, bf16[4,4,288,128]{3,0,2,1:T(4,128)(2,1)S(1)}, u32[]{:S(2)}, u32[]{:S(2)}) collective-permute-start(bf16[4,4,288,128]{3,0,2,1:T(4,128)(2,1)S(1)} %broadcast_select_fusion.1), channel_id=1, source_target_pairs={{0,4},{1,5},{2,6},{3,7},{4,8},{5,9},{6,10},{7,11},{8,12},{9,13},{1... | collective-permute-start | bytes 3538952 | tf_op jit(solution)/shard_map/ppermute | solution.py:11
  96.4 3.9 %copy-start.1 = (s32[64]{0:T(128)S(1)}, s32[64]{0:T(128)}, u32[]{:S(2)}) copy-start(s32[64]{0:T(128)} %param.6) | copy-start | bytes 772
  96.4 4.0 %copy-start.2 = (s32[64]{0:T(128)S(1)}, s32[64]{0:T(128)}, u32[]{:S(2)}) copy-start(s32[64]{0:T(128)} %param.5) | copy-start | bytes 772
  97.2 25.3 %collective-permute-start.3 = (bf16[4,4,288,128]{3,0,2,1:T(4,128)(2,1)S(1)}, bf16[4,4,288,128]{3,0,2,1:T(4,128)(2,1)S(1)}, u32[]{:S(2)}, u32[]{:S(2)}) collective-permute-start(bf16[4,4,288,128]{3,0,2,1:T(4,128)(2,1)S(1)} %broadcast_select_fusion.2), channel_id=1, source_target_pairs={{0,8},{1,9},{2,10},{3,11},{4,12},{5,13},{6,14},{7,15},{8,0},{9,1},... | collective-permute-start | bytes 3538952 | tf_op jit(solution)/shard_map/ppermute | solution.py:11
  244.5 17.8 %copy-start = (f32[4,4]{1,0:T(4,128)}, f32[4,4]{1,0:T(4,128)S(1)}, u32[]{:S(2)}) copy-start(f32[4,4]{1,0:T(4,128)S(1)} %reduce_max.18) | copy-start | bytes 196
Sparse Core Ops, SparseCore 0:
  124.9 112.0 all-gather.1
where the time goes:
time: 287 us
  waiting for transfers between devices  211 us (74%)
  other arithmetic  28.6 us (10%)
  matrix products  17 us (6%)
  between operations  14.1 us (5%)
  starting transfers between devices  8.35 us (3%)
  local copies, waits for them, and re-layouts  7.23 us (3%)
    all_gather x1, waiting for transfers between devices, per_device(): lax.all_gather(block_part.reshape(layers, rows_here, per_col * HDIM), 'ro...  112 us
    ppermute x4, waiting for transfers between devices, passed_along(): lax.ppermute(shard, axis, [(i, (i + by) % devices) for i in range(devices)])  99.2 us
    convert_element_type x1, other arithmetic, per_device(): (joined_four.astype(jnp.float32) / (peaks[:, None, :, None] + 1e-06)).ast...  17.7 us
    dot_general x1, matrix products, per_device(): jnp.einsum('td,lde->lte', probe, codes, preferred_element_type=jnp.float32)  15.2 us
    ppermute x4, starting transfers between devices, passed_along(): lax.ppermute(shard, axis, [(i, (i + by) % devices) for i in range(devices)])  8.31 us
    reduce_max x2, other arithmetic, per_device(): peaks = jnp.max(jnp.abs(joined_four.astype(jnp.float32)), axis=(1, 3))  7.46 us
  transfers between devices with their start and end apart: 5, of which 5 were waited for; matrix products, arithmetic and copies ran while one was open for 0% of the time, Pallas kernels for 0%

commit v1 on v0

v1 whole, which is shorter than its diff:
```python
import functools

import jax
import jax.numpy as jnp
from jax import lax
from jax.experimental import pallas as pl
from jax.experimental.pallas import tpu as pltpu
from jax.sharding import PartitionSpec as P

HDIM = 128
MESH = pl.DeviceIdType.MESH
LAYERS = 4
NZ = 8
NCOL = 16
HEADS = 64
PER = 4
EPS = 1e-06


def rem(a, n):
    return lax.rem(a, n)


def send_classes(src_ref, tgt_ref, col):
    heads = [src_ref[col * PER + i] for i in range(PER)]

    def look(t, found):
        head = tgt_ref[t]
        return tuple(jnp.where(head == h, t, f) for h, f in zip(heads, found))

    zero = jnp.int32(0)
    found = lax.fori_loop(0, HEADS, look, (zero,) * PER, unroll=8)
    shifts = [rem(f // PER - col + NCOL, NCOL) for f in found]

    def first(test):
        at = jnp.int32(PER - 1)
        for i in range(PER - 2, -1, -1):
            at = jnp.where(test(shifts[i]), i, at)
        return at

    at_a = first(lambda s: s == 8)
    at_b = first(lambda s: s == 1)
    at_s = first(lambda s: (s != 8) & (s != 1))
    at_e = 6 - at_a - at_b - at_s

    def pick(at):
        value = shifts[PER - 1]
        for i in range(PER - 2, -1, -1):
            value = jnp.where(at == i, shifts[i], value)
        return value

    return at_a, at_b, at_s, at_e, pick(at_s), pick(at_e)


def recv_classes(src_ref, tgt_ref, col):
    wanted = [tgt_ref[col * PER + j] for j in range(PER)]

    def look(t, found):
        head = src_ref[t]
        return tuple(jnp.where(head == h, t, f) for h, f in zip(wanted, found))

    zero = jnp.int32(0)
    found = lax.fori_loop(0, HEADS, look, (zero,) * PER, unroll=8)
    classes = []
    for f in found:
        from_col = f // PER
        place = rem(f, PER)
        shift = rem(col - from_col + NCOL, NCOL)
        later = jnp.int32(0)
        for i in range(PER - 1):
            head = src_ref[from_col * PER + i]
            mine = jnp.int32(0)
            for h in wanted:
                mine = jnp.where(head == h, 1, mine)
            later = jnp.where(i < place, jnp.maximum(later, mine), later)
        kind = jnp.where(shift == 8, 0, jnp.where(shift == 1, 1, 2))
        classes.append(jnp.where(later == 1, 3, kind))
    return classes


def gather_kernel(
    src_ref, tgt_ref, w_hbm, probe_hbm,
    c_ref, acc_ref, pk_ref,
    g_ref, probe_ref, w_ref, sb_ref, mx_ref, mine_ref, rk_ref,
    x1a, x1b, x1c, x1d, x2a, x2b, x2c, x2d,
    y1a, y1b, y1c, y1d, y2a, y2b, y2c, y2d,
    w_sem, p_sem, ab_recv, ab_send, xy_recv, xy_send, z_recv, z_send,
    own_recv, own_send, d_recv, d_send, mx_recv, mx_send,
):
    x1, x2 = (x1a, x1b, x1c, x1d), (x2a, x2b, x2c, x2d)
    y1, y2 = (y1a, y1b, y1c, y1d), (y2a, y2b, y2c, y2d)
    row = lax.axis_index("row")
    col = lax.axis_index("col")
    z, core = row // 2, rem(row, 2)
    depth = w_ref.shape[1]
    quad = 4 * depth

    def w_copy(l):
        return pltpu.make_async_copy(w_hbm.at[l], w_ref.at[l], w_sem.at[l])

    def p_copy():
        return pltpu.make_async_copy(probe_hbm, probe_ref, p_sem)

    barrier = pltpu.get_barrier_semaphore()
    for d in range(1, 16):
        pl.semaphore_signal(barrier, inc=1, device_id=(rem(row + d, 16), col), device_id_type=MESH)
    for d in (8, 1, 15, 4, 12):
        pl.semaphore_signal(barrier, inc=1, device_id=(row, rem(col + d, NCOL)), device_id_type=MESH)
    for l in range(LAYERS):
        w_copy(l).start()
    p_copy().start()

    at_a, at_b, at_s, at_e, s_by, e_by = send_classes(src_ref, tgt_ref, col)
    s_x, s_y = rem((s_by + 1) // 4, 4), rem(s_by + 1, 4) - 1
    e_x, e_y = rem((e_by + 2) // 4, 4), rem(e_by + 2, 4) - 2
    x1_s = jnp.where(s_x == 0, 0, jnp.where(s_x == 3, 2, 1))
    x1_e = jnp.where(e_x == 0, 0, jnp.where(e_x == 1, 1, 2))
    x2_s, x2_e = jnp.where(s_x == 2, 1, 0), jnp.where(e_x == 2, 1, 0)
    y1_s = jnp.where(s_y == 0, 0, jnp.where(s_y == -1, 2, 1))
    y1_e = jnp.where(e_y == 0, 0, jnp.where(e_y == 1, 1, 2))
    y2_s, y2_e = jnp.where(s_y == 2, 1, 0), jnp.where(e_y == -2, 1, 0)

    def choose(at, values):
        out = values[-1]
        for i in range(len(values) - 2, -1, -1):
            out = jnp.where(at == i, values[i], out)
        return out

    def head(l, at):
        return choose(at, [w_ref[l, :, i * HDIM:(i + 1) * HDIM] for i in range(PER)])

    for l in range(LAYERS):
        w_copy(l).wait()
        sb_ref[l, 0] = head(l, at_a)
        sb_ref[l, 1] = head(l, at_b)
        x1[l][0, 0] = head(l, at_s)
        x1[l][0, 1] = head(l, at_e)

    pl.semaphore_wait(barrier, 20)

    def to_col(src, dst, sems, at, by):
        send, recv = sems
        return pltpu.make_async_remote_copy(
            src_ref=src, dst_ref=dst, send_sem=send.at[at], recv_sem=recv.at[at],
            device_id=(row, rem(col + by, NCOL)), device_id_type=MESH,
        )

    def a_copy(l):
        return to_col(sb_ref.at[l, 0], g_ref.at[0, 0, l, 0], (ab_send, ab_recv), (l, 0), 8)

    def b_copy(l):
        return to_col(sb_ref.at[l, 1], g_ref.at[0, 0, l, 1], (ab_send, ab_recv), (l, 1), 1)

    def x1_copy(l, way):
        return to_col(x1[l].at[0], x1[l].at[1 + way], (xy_send, xy_recv), (0, l, way), (4, 12)[way])

    def x2_copy(l, half):
        return to_col(x2[l].at[0, half], x2[l].at[1, half], (xy_send, xy_recv), (1, l, half), (4, 12)[half])

    def y1_copy(l, way):
        return to_col(y1[l].at[0], y1[l].at[1 + way], (xy_send, xy_recv), (2, l, way), (1, 15)[way])

    def y2_copy(l, half):
        return to_col(y2[l].at[0, half], y2[l].at[1, half], (xy_send, xy_recv), (3, l, half), (1, 15)[half])

    for l in range(LAYERS):
        a_copy(l).start()
        b_copy(l).start()
    for l in range(LAYERS):
        for way in range(2):
            x1_copy(l, way).start()

    def z_copy(way, d, q, slot):
        to = rem(z + (1, NZ - 1)[way], NZ) * 2 + core
        return pltpu.make_async_remote_copy(
            src_ref=g_ref.at[d, 0, q], dst_ref=g_ref.at[(d + (NZ - 1, 1)[way]) % NZ, 0, q],
            send_sem=z_send.at[way, slot], recv_sem=z_recv.at[way, slot],
            device_id=(to, col), device_id_type=MESH,
        )

    def z_arrival(way, d, q, slot):
        return z_copy(way, (d + (1, NZ - 1)[way]) % NZ, q, slot)

    def d_copy(d, q, sems, at):
        send, recv = sems
        return pltpu.make_async_remote_copy(
            src_ref=g_ref.at[d, 0, q], dst_ref=g_ref.at[d, 1, q],
            send_sem=send.at[at], recv_sem=recv.at[at],
            device_id=(z * 2 + 1 - core, col), device_id_type=MESH,
        )

    def d_own(q):
        return d_copy(0, q, (own_send, own_recv), q)

    def d_passed(way, slot, d, q):
        return d_copy(d, q, (d_send, d_recv), (way, slot))

    def send_own(q):
        for way in range(2):
            z_copy(way, 0, q, q // 4 * 14 + q % 4).start()
        d_own(q).start()

    def place(way, slot):
        group, i = slot // 14, slot % 14
        hop = i // 4 + 1
        q = group * 4 + (i % 4 if i < 12 else 2 * (i - 12) + way)
        return (NZ - hop, hop)[way], q

    def ring(slot):
        i = slot % 14
        for way in range(2):
            d, q = place(way, slot)
            z_arrival(way, d, q, slot).wait_recv()
            if i < 8:
                z_copy(way, d, q, slot + 4).start()
            elif i < 12 and i % 2 == way:
                z_copy(way, d, q, slot - i + 12 + (i - 8) // 2).start()
            d_passed(way, slot, d, q).start()

    def beside(slot):
        for way in range(2):
            d_passed(way, slot, *place(way, slot)).wait_recv()

    def biggest(group):
        rows = []
        for half in range(2):
            for l in range(LAYERS):
                block = g_ref[0, 0, group * 4 + l, half]
                rows.append(jnp.max(jnp.abs(block.astype(jnp.float32)), axis=0, keepdims=True))
        mine_ref[group] = jnp.concatenate(rows, axis=0)

    def mx_copy(group, by):
        return pltpu.make_async_remote_copy(
            src_ref=mine_ref.at[group], dst_ref=mx_ref.at[group, by],
            send_sem=mx_send.at[group, by], recv_sem=mx_recv.at[group, by],
            device_id=(rem(row + by, 16), col), device_id_type=MESH,
        )

    def settle(group):
        for by in range(1, 16):
            mx_copy(group, by).wait_recv()
        top = mine_ref[group]
        for rb in range(1, 16):
            top = jnp.maximum(top, mx_ref[group, rb])
        top = jnp.broadcast_to(jnp.max(top, axis=1, keepdims=True), top.shape)
        pk_ref[group] = top
        rk_ref[group] = 1.0 / ((top + EPS) * 0.0625)

    even = rem(z, 2) == 0

    def unit(group, t, l):
        p = rem(z // 2 + (0, -1, 1, 2)[t] * (1 - 2 * rem(z, 2)) + 4, 4)
        q = group * 4 + l
        start = pl.multiple_of(p * quad, HDIM)
        for half in range(2):
            scale = rk_ref[group, half * 4 + l:half * 4 + l + 1, :]
            for d in ((0, 1), (-1, -2), (2, 3), (-3, 4))[t]:
                for other in range(2):
                    block = g_ref[d % NZ, other, q, half]
                    if d % 4:
                        block = jnp.where(even, block, g_ref[-d % NZ, other, q, half])
                    at = start + rem(z + d + NZ, 2) * (2 * depth) + (core + other - 2 * core * other) * depth
                    c_ref[q, half, pl.ds(pl.multiple_of(at, 16), depth), :] = (
                        (block.astype(jnp.float32) * 0.0625) * scale
                    ).astype(jnp.bfloat16)
        both = jnp.concatenate(
            [c_ref[q, 0, pl.ds(start, quad), :], c_ref[q, 1, pl.ds(start, quad), :]], axis=1
        )
        acc_ref[q] += jnp.dot(
            probe_ref[:, pl.ds(start, quad)], both, preferred_element_type=jnp.float32
        )

    for l in range(LAYERS):
        for half, copy in enumerate((a_copy, b_copy)):
            copy(l).wait_recv()
        send_own(l)

    @pl.loop(0, 8)
    def _(q):
        acc_ref[q] = jnp.zeros(acc_ref.shape[1:], jnp.float32)

    biggest(0)

    for i in range(15):
        if i == 1:
            for by in range(1, 16):
                mx_copy(0, by).start()
        l = i - 4
        sends = []
        if 0 <= l < 4:
            for way in range(2):
                x1_copy(l, way).wait_recv()
            x2[l][0, 0] = choose(x1_s, [x1[l][i, 0] for i in range(3)])
            x2[l][0, 1] = choose(x1_e, [x1[l][i, 1] for i in range(3)])
            sends += [x2_copy(l, 0), x2_copy(l, 1)]
        l = i - 7
        if 0 <= l < 4:
            for half in range(2):
                x2_copy(l, half).wait_recv()
            y1[l][0, 0] = choose(x2_s, [x2[l][i, 0] for i in range(2)])
            y1[l][0, 1] = choose(x2_e, [x2[l][i, 1] for i in range(2)])
            sends += [y1_copy(l, 0), y1_copy(l, 1)]
        l = i - 9
        if 0 <= l < 4:
            for way in range(2):
                y1_copy(l, way).wait_recv()
            y2[l][0, 0] = choose(y1_s, [y1[l][i, 0] for i in range(3)])
            y2[l][0, 1] = choose(y1_e, [y1[l][i, 1] for i in range(3)])
            sends += [y2_copy(l, 0), y2_copy(l, 1)]
        l = i - 11
        own = None
        if 0 <= l < 4:
            for half in range(2):
                y2_copy(l, half).wait_recv()
            g_ref[0, 0, 4 + l, 0] = choose(y2_s, [y2[l][i, 0] for i in range(2)])
            g_ref[0, 0, 4 + l, 1] = choose(y2_e, [y2[l][i, 1] for i in range(2)])
            own = 4 + l
        if i > 0:
            beside(i - 1)
        for copy in sends:
            copy.start()
        if own is not None:
            send_own(own)
        ring(i)

    p_copy().wait()
    biggest(1)
    settle(0)
    for q in range(4):
        d_own(q).wait_recv()

    for by in range(1, 16):
        mx_copy(1, by).start()

    def units(group, t, first, last):
        for l in range(first, last):
            unit(group, t, l)

    work = {15: (0, 0, 0, 4), 16: (0, 1, 0, 4), 17: (0, 2, 0, 4), 18: (0, 3, 0, 4)}
    work.update({21: (1, 0, 0, 4), 22: (1, 1, 0, 4), 24: (1, 2, 0, 2), 26: (1, 2, 2, 4)})
    work.update({27: (1, 3, 0, 2), 28: (1, 3, 2, 4)})
    for slot in range(15, 29):
        beside(slot - 1)
        if slot < 28:
            ring(slot)
        if slot == 21:
            settle(1)
            for q in range(4, 8):
                d_own(q).wait_recv()
        if slot in work:
            units(*work[slot])

    for q in range(8):
        d_own(q).wait_send()
    for slot in range(28):
        for way in range(2):
            d, q = place(way, slot)
            d_passed(way, slot, d, q).wait_send()
            z_arrival(way, d, q, slot).wait_send()
    for l in range(LAYERS):
        a_copy(l).wait_send()
        b_copy(l).wait_send()
        for way in range(2):
            x1_copy(l, way).wait_send()
            x2_copy(l, way).wait_send()
            y1_copy(l, way).wait_send()
            y2_copy(l, way).wait_send()
    for group in range(2):
        for by in range(1, 16):
            mx_copy(group, by).wait_send()


def output_kernel(
    src_ref, tgt_ref, c_ref, acc_ref, pk_ref,
    codes_hbm, peaks_ref, checked_hbm,
    chk_ref, sem, chk_sem,
):
    col = lax.axis_index("col")
    classes = recv_classes(src_ref, tgt_ref, col)
    slots = []
    for c in range(4):
        at = jnp.int32(0)
        for j in range(1, PER):
            at = jnp.where(classes[j] == c, j, at)
        slots.append(at)

    def lanes(c):
        return pl.ds(pl.multiple_of(slots[c] * HDIM, HDIM), HDIM)

    copies = []
    for l in range(LAYERS):
        for c in range(4):
            copy = pltpu.make_async_copy(
                c_ref.at[c // 2 * 4 + l, c % 2], codes_hbm.at[l, :, lanes(c)], sem.at[l, c]
            )
            copy.start()
            copies.append(copy)
    for l in range(LAYERS):
        for c in range(4):
            half = c % 2
            scale = pk_ref[c // 2, half * 4 + l:half * 4 + l + 1, :]
            block = acc_ref[c // 2 * 4 + l, :, half * HDIM:(half + 1) * HDIM]
            chk_ref[l, c] = (block * scale).astype(jnp.bfloat16)
            copy = pltpu.make_async_copy(
                chk_ref.at[l, c], checked_hbm.at[l, :, lanes(c)], chk_sem.at[l, c]
            )
            copy.start()
            copies.append(copy)
    lane = lax.broadcasted_iota(jnp.int32, (LAYERS, HDIM), 1)
    out = jnp.zeros((LAYERS, HDIM), jnp.float32)
    for c in range(4):
        half = c % 2
        out = jnp.where(lane == slots[c], pk_ref[c // 2, half * 4:half * 4 + 4, :], out)
    peaks_ref[...] = out[:, :PER]
    for copy in copies:
        copy.wait()


def per_device(train_weight, src_map, tgt_map, probe):
    layers, depth, width = train_weight.shape
    tokens, model = probe.shape
    bf16, f32 = jnp.bfloat16, jnp.float32
    smem = pl.BlockSpec(memory_space=pltpu.SMEM)
    vmem = pl.BlockSpec(memory_space=pltpu.VMEM)
    hbm = pl.BlockSpec(memory_space=pl.ANY)
    three = pltpu.VMEM((3, 2, depth, HDIM), bf16)
    two = pltpu.VMEM((2, 2, depth, HDIM), bf16)
    dma = pltpu.SemaphoreType.DMA
    c, acc, pk = pl.pallas_call(
        gather_kernel,
        name="gather_codes",
        out_shape=(
            pltpu.VMEM((8, 2, model, HDIM), bf16),
            pltpu.VMEM((8, tokens, 2 * HDIM), f32),
            pltpu.VMEM((2, 8, HDIM), f32),
        ),
        in_specs=[smem, smem, hbm, hbm],
        out_specs=(vmem, vmem, vmem),
        scratch_shapes=[
            pltpu.VMEM((NZ, 2, 8, 2, depth, HDIM), bf16),
            pltpu.VMEM((tokens, model), bf16),
            pltpu.VMEM((layers, depth, width), bf16),
            pltpu.VMEM((layers, 2, depth, HDIM), bf16),
            pltpu.VMEM((2, 16, 8, HDIM), f32),
            pltpu.VMEM((2, 8, HDIM), f32),
            pltpu.VMEM((2, 8, HDIM), f32),
        ]
        + [three] * 4 + [two] * 4 + [three] * 4 + [two] * 4
        + [
            dma((4,)), dma, dma((4, 2)), dma((4, 2)), dma((4, 4, 2)), dma((4, 4, 2)),
            dma((2, 28)), dma((2, 28)), dma((8,)), dma((8,)), dma((2, 28)), dma((2, 28)),
            dma((2, 16)), dma((2, 16)),
        ],
        compiler_params=pltpu.CompilerParams(
            collective_id=0, has_side_effects=True, vmem_limit_bytes=36 * 1024 * 1024
        ),
    )(src_map, tgt_map, train_weight, probe)
    return pl.pallas_call(
        output_kernel,
        name="write_outputs",
        out_shape=(
            jax.ShapeDtypeStruct((layers, model, width), bf16),
            jax.ShapeDtypeStruct((layers, PER), f32),
            jax.ShapeDtypeStruct((layers, tokens, width), bf16),
        ),
        in_specs=[smem, smem, vmem, vmem, vmem],
        out_specs=(hbm, vmem, hbm),
        scratch_shapes=[
            pltpu.VMEM((layers, 4, tokens, HDIM), bf16),
            dma((4, 4)),
            dma((4, 4)),
        ],
        compiler_params=pltpu.CompilerParams(vmem_limit_bytes=8 * 1024 * 1024),
    )(src_map, tgt_map, c, acc, pk)


def solution(mesh):
    in_specs = (P(None, "row", "col"), P(), P(), P("row", None))
    out_specs = (P(None, None, "col"), P(None, "col"), P(None, "row", "col"))
    return jax.shard_map(
        per_device, mesh=mesh, in_specs=in_specs, out_specs=out_specs, check_vma=False
    )
```

time: 287 us -> 129 us (0.45)
  waiting for transfers between devices: 211 us -> 0 us
  Pallas kernels: 0 us -> 128 us
  other arithmetic: 28.6 us -> 0 us
  matrix products: 17 us -> 0 us
  between operations: 14.1 us -> 0.83 us
  starting transfers between devices: 8.35 us -> 0 us
  local copies, waits for them, and re-layouts: 7.23 us -> 0.01 us
    pallas_call x0 -> x2, Pallas kernels: none -> 128 us  [the longest x1 119 us: per_device(): pl.pallas_call(gather_kernel, name='gather_codes', out_shape=(pltpu.VMEM(...]
    all_gather x1 -> x0, waiting for transfers between devices: 112 us -> none  [per_device(): lax.all_gather(block_part.reshape(layers, rows_here, per_col * HDIM), 'ro...]
    ppermute x4 -> x0, waiting for transfers between devices: 99.2 us -> none  [passed_along(): lax.ppermute(shard, axis, [(i, (i + by) % devices) for i in range(devices)])]
    convert_element_type x1 -> x0, other arithmetic: 17.7 us -> none  [per_device(): (joined_four.astype(jnp.float32) / (peaks[:, None, :, None] + 1e-06)).ast...]
    dot_general x3 -> x0, matrix products: 17 us -> none  [the longest x1 15.2 us: per_device(): jnp.einsum('td,lde->lte', probe, codes, preferred_element_type=jnp.float32)]
    ppermute x4 -> x0, starting transfers between devices: 8.31 us -> none  [passed_along(): lax.ppermute(shard, axis, [(i, (i + by) % devices) for i in range(devices)])]
    reduce_max x2 -> x0, other arithmetic: 7.46 us -> none  [per_device(): peaks = jnp.max(jnp.abs(joined_four.astype(jnp.float32)), axis=(1, 3))]
    reshape x2 -> x0, local copies, waits for them, and re-layouts: 3.83 us -> none  [the longest x1 2.53 us: per_device(): local_four = train_weight.reshape(layers, rows_here, per_col, HDIM)]
  transfers between devices with their start and end apart: 5 -> 0, of which waited for: 5 -> 0; matrix products, arithmetic and copies ran while one was open for 0% -> 0% of each run, Pallas kernels for 0% -> 0%
where the time goes in v1:
time: 129 us
  Pallas kernels  128 us (99%)
    pallas_call x1, Pallas kernels, per_device(): pl.pallas_call(gather_kernel, name='gather_codes', out_shape=(pltpu.VMEM(...  119 us
    pallas_call x1, Pallas kernels, per_device(): pl.pallas_call(output_kernel, name='write_outputs', out_shape=(jax.ShapeD...  8.79 us

profile of v1, /device:TPU:1, one launch (start us, length us, event | category | flops | bytes accessed | tf_op | source)
XLA Modules:
  0.0 128.7 jit_solution(138825509983958938)
XLA Ops:
  0.6 0.0 copy-start.1
  0.6 0.0 copy-start
  0.7 119.1 %gather_codes.1 = (bf16[8,2,4608,128]{3,2,1,0:T(8,128)(2,1)S(1)}, f32[8,512,256]{2,1,0:T(8,128)S(1)}, f32[2,8,128]{2,1,0:T(8,128)S(1)}) custom-call(s32[64]{0:T(128)} %src_ref.3, s32[64]{0:T(128)} %tgt_ref.3, bf16[4,288,512]{2,1,0:T(8,128)(2,1)} %w_hbm.1, bf16[512,4608]{1,0:T(8,128)(2,1)} %probe_hbm.1), custom_call_target="tpu_custom_call" | custom-call | tf_op jit(solution)/shard_map/gather_codes/pallas_call | solution.py:429
  119.7 0.0 copy-done.1
  119.7 0.0 copy-done
  119.7 8.8 %write_outputs.1 = (bf16[4,4608,512]{2,1,0:T(8,128)(2,1)}, f32[4,4]{1,0:T(4,128)}, bf16[4,512,512]{2,1,0:T(8,128)(2,1)}) custom-call(s32[64]{0:T(128)S(1)} %copy-done, s32[64]{0:T(128)S(1)} %copy-done.1, bf16[8,2,4608,128]{3,2,1,0:T(8,128)(2,1)S(1)} %get-tuple-element.6.c_ref, f32[8,512,256]{2,1,0:T(8,128)S(1)} %get-tuple-element.7.acc_ref, ...), custom_call_target="tpu_custom_call" | custom-call | tf_op jit(solution)/shard_map/write_outputs/pallas_call | solution.py:458
Async XLA Ops:
  0.6 119.1 %copy-start.1 = (s32[64]{0:T(128)S(1)}, s32[64]{0:T(128)}, u32[]{:S(2)}) copy-start(s32[64]{0:T(128)} %tgt_ref.3) | copy-start | bytes 772
  0.6 119.1 %copy-start = (s32[64]{0:T(128)S(1)}, s32[64]{0:T(128)}, u32[]{:S(2)}) copy-start(s32[64]{0:T(128)} %src_ref.3) | copy-start | bytes 772

commit v2 on v1

--- a/solution.py
+++ b/solution.py
@@ -80,12 +80,12 @@
 
 def gather_kernel(
     src_ref, tgt_ref, w_hbm, probe_hbm,
-    c_ref, acc_ref, pk_ref,
+    c_ref, acc_ref, pk_ref, last_ref,
     g_ref, probe_ref, w_ref, sb_ref, mx_ref, mine_ref, rk_ref,
     x1a, x1b, x1c, x1d, x2a, x2b, x2c, x2d,
     y1a, y1b, y1c, y1d, y2a, y2b, y2c, y2d,
-    w_sem, p_sem, ab_recv, ab_send, xy_recv, xy_send, z_recv, z_send,
-    own_recv, own_send, d_recv, d_send, mx_recv, mx_send,
+    w_sem, p_sem, ab_recv, xy_recv, z_recv, own_recv, d_recv, mx_recv,
+    xy_send, z_send, d_send, mx_send,
 ):
     x1, x2 = (x1a, x1b, x1c, x1d), (x2a, x2b, x2c, x2d)
     y1, y2 = (y1a, y1b, y1c, y1d), (y2a, y2b, y2c, y2d)
@@ -136,69 +136,71 @@
         x1[l][0, 0] = head(l, at_s)
         x1[l][0, 1] = head(l, at_e)
 
+    @pl.loop(0, 8)
+    def _(q):
+        acc_ref[q] = jnp.zeros(acc_ref.shape[1:], jnp.float32)
+
     pl.semaphore_wait(barrier, 20)
 
-    def to_col(src, dst, sems, at, by):
-        send, recv = sems
+    def total(part, send, recv):
         return pltpu.make_async_remote_copy(
-            src_ref=src, dst_ref=dst, send_sem=send.at[at], recv_sem=recv.at[at],
+            src_ref=part, dst_ref=part, send_sem=send, recv_sem=recv,
+            device_id=(row, rem(col + 1, NCOL)), device_id_type=MESH,
+        )
+
+    def to_col(src, dst, recv, by):
+        return pltpu.make_async_remote_copy(
+            src_ref=src, dst_ref=dst, send_sem=xy_send, recv_sem=recv,
             device_id=(row, rem(col + by, NCOL)), device_id_type=MESH,
         )
 
     def a_copy(l):
-        return to_col(sb_ref.at[l, 0], g_ref.at[0, 0, l, 0], (ab_send, ab_recv), (l, 0), 8)
+        return to_col(sb_ref.at[l, 0], g_ref.at[0, 0, 2 + l // 2, l % 2], ab_recv.at[l, 0], 8)
 
     def b_copy(l):
-        return to_col(sb_ref.at[l, 1], g_ref.at[0, 0, l, 1], (ab_send, ab_recv), (l, 1), 1)
-
-    def x1_copy(l, way):
-        return to_col(x1[l].at[0], x1[l].at[1 + way], (xy_send, xy_recv), (0, l, way), (4, 12)[way])
-
-    def x2_copy(l, half):
-        return to_col(x2[l].at[0, half], x2[l].at[1, half], (xy_send, xy_recv), (1, l, half), (4, 12)[half])
-
-    def y1_copy(l, way):
-        return to_col(y1[l].at[0], y1[l].at[1 + way], (xy_send, xy_recv), (2, l, way), (1, 15)[way])
-
-    def y2_copy(l, half):
-        return to_col(y2[l].at[0, half], y2[l].at[1, half], (xy_send, xy_recv), (3, l, half), (1, 15)[half])
-
-    for l in range(LAYERS):
+        return to_col(sb_ref.at[l, 1], g_ref.at[0, 0, l // 2, l % 2], ab_recv.at[l, 1], 1)
+
+    def wide_copy(stage, buffer, l, way, by):
+        return to_col(buffer[l].at[0], buffer[l].at[1 + way], xy_recv.at[stage, l], by[way])
+
+    def half_copy(stage, buffer, l, half, by):
+        return to_col(buffer[l].at[0, half], buffer[l].at[1, half], xy_recv.at[stage, l], by[half])
+
+    def shifted(stage, buffer, l):
+        part = buffer[l].at[pl.ds(0, 2)] if stage % 2 == 0 else buffer[l].at[0]
+        total(part, xy_send, xy_recv.at[stage, l]).wait_recv()
+
+    for l in range(LAYERS):
+        b_copy(l).start()
         a_copy(l).start()
-        b_copy(l).start()
     for l in range(LAYERS):
         for way in range(2):
-            x1_copy(l, way).start()
-
-    def z_copy(way, d, q, slot):
+            wide_copy(0, x1, l, way, (4, 12)).start()
+
+    def z_copy(way, d, at, slot):
         to = rem(z + (1, NZ - 1)[way], NZ) * 2 + core
         return pltpu.make_async_remote_copy(
-            src_ref=g_ref.at[d, 0, q], dst_ref=g_ref.at[(d + (NZ - 1, 1)[way]) % NZ, 0, q],
-            send_sem=z_send.at[way, slot], recv_sem=z_recv.at[way, slot],
+            src_ref=g_ref.at[(d, 0) + at], dst_ref=g_ref.at[((d + (NZ - 1, 1)[way]) % NZ, 0) + at],
+            send_sem=z_send, recv_sem=z_recv.at[slot],
             device_id=(to, col), device_id_type=MESH,
         )
 
-    def z_arrival(way, d, q, slot):
-        return z_copy(way, (d + (1, NZ - 1)[way]) % NZ, q, slot)
-
-    def d_copy(d, q, sems, at):
-        send, recv = sems
+    def d_copy(d, q, recv):
         return pltpu.make_async_remote_copy(
             src_ref=g_ref.at[d, 0, q], dst_ref=g_ref.at[d, 1, q],
-            send_sem=send.at[at], recv_sem=recv.at[at],
+            send_sem=d_send, recv_sem=recv,
             device_id=(z * 2 + 1 - core, col), device_id_type=MESH,
         )
 
-    def d_own(q):
-        return d_copy(0, q, (own_send, own_recv), q)
-
-    def d_passed(way, slot, d, q):
-        return d_copy(d, q, (d_send, d_recv), (way, slot))
-
-    def send_own(q):
+    def send_own(q, half=None):
+        at = (q,) if half is None else (q, half)
         for way in range(2):
-            z_copy(way, 0, q, q // 4 * 14 + q % 4).start()
-        d_own(q).start()
+            z_copy(way, 0, at, q // 4 * 14 + q % 4).start()
+        if half != 0:
+            d_copy(0, q, own_recv.at[q // 4]).start()
+
+    def own_beside(group):
+        total(g_ref.at[0, 0, pl.ds(0, 4)], d_send, own_recv.at[group]).wait_recv()
 
     def place(way, slot):
         group, i = slot // 14, slot % 14
@@ -208,18 +210,19 @@
 
     def ring(slot):
         i = slot % 14
+        total(g_ref.at[0, 0, pl.ds(0, 2)], z_send, z_recv.at[slot]).wait_recv()
         for way in range(2):
             d, q = place(way, slot)
-            z_arrival(way, d, q, slot).wait_recv()
             if i < 8:
-                z_copy(way, d, q, slot + 4).start()
+                z_copy(way, d, (q,), slot + 4).start()
             elif i < 12 and i % 2 == way:
-                z_copy(way, d, q, slot - i + 12 + (i - 8) // 2).start()
-            d_passed(way, slot, d, q).start()
+                z_copy(way, d, (q,), slot - i + 12 + (i - 8) // 2).start()
+        for way in range(2):
+            d, q = place(way, slot)
+            d_copy(d, q, d_recv.at[slot]).start()
 
     def beside(slot):
-        for way in range(2):
-            d_passed(way, slot, *place(way, slot)).wait_recv()
+        total(g_ref.at[0, 0, pl.ds(0, 2)], d_send, d_recv.at[slot]).wait_recv()
 
     def biggest(group):
         rows = []
@@ -232,13 +235,12 @@
     def mx_copy(group, by):
         return pltpu.make_async_remote_copy(
             src_ref=mine_ref.at[group], dst_ref=mx_ref.at[group, by],
-            send_sem=mx_send.at[group, by], recv_sem=mx_recv.at[group, by],
+            send_sem=mx_send, recv_sem=mx_recv.at[group],
             device_id=(rem(row + by, 16), col), device_id_type=MESH,
         )
 
     def settle(group):
-        for by in range(1, 16):
-            mx_copy(group, by).wait_recv()
+        total(mx_ref.at[group, pl.ds(1, 15)], mx_send, mx_recv.at[group]).wait_recv()
         top = mine_ref[group]
         for rb in range(1, 16):
             top = jnp.maximum(top, mx_ref[group, rb])
@@ -263,6 +265,8 @@
                     c_ref[q, half, pl.ds(pl.multiple_of(at, 16), depth), :] = (
                         (block.astype(jnp.float32) * 0.0625) * scale
                     ).astype(jnp.bfloat16)
+        if group == 1 and t == 3:
+            return
         both = jnp.concatenate(
             [c_ref[q, 0, pl.ds(start, quad), :], c_ref[q, 1, pl.ds(start, quad), :]], axis=1
         )
@@ -270,53 +274,54 @@
             probe_ref[:, pl.ds(start, quad)], both, preferred_element_type=jnp.float32
         )
 
-    for l in range(LAYERS):
-        for half, copy in enumerate((a_copy, b_copy)):
-            copy(l).wait_recv()
-        send_own(l)
-
-    @pl.loop(0, 8)
-    def _(q):
-        acc_ref[q] = jnp.zeros(acc_ref.shape[1:], jnp.float32)
-
+    def took(kind, l):
+        (a_copy, b_copy)[kind](l).wait_recv()
+        send_own(2 * (1 - kind) + l // 2, l % 2)
+
+    took(1, 0)
+    took(1, 1)
+    took(0, 0)
+    took(1, 2)
+    took(1, 3)
+    took(0, 1)
+    ring(0)
+    took(0, 2)
+    beside(0)
+    ring(1)
+    took(0, 3)
     biggest(0)
 
-    for i in range(15):
-        if i == 1:
+    for i in range(2, 15):
+        if i == 3:
             for by in range(1, 16):
                 mx_copy(0, by).start()
         l = i - 4
         sends = []
         if 0 <= l < 4:
-            for way in range(2):
-                x1_copy(l, way).wait_recv()
-            x2[l][0, 0] = choose(x1_s, [x1[l][i, 0] for i in range(3)])
-            x2[l][0, 1] = choose(x1_e, [x1[l][i, 1] for i in range(3)])
-            sends += [x2_copy(l, 0), x2_copy(l, 1)]
+            shifted(0, x1, l)
+            x2[l][0, 0] = choose(x1_s, [x1[l][k, 0] for k in range(3)])
+            x2[l][0, 1] = choose(x1_e, [x1[l][k, 1] for k in range(3)])
+            sends += [half_copy(1, x2, l, half, (4, 12)) for half in range(2)]
         l = i - 7
         if 0 <= l < 4:
-            for half in range(2):
-                x2_copy(l, half).wait_recv()
-            y1[l][0, 0] = choose(x2_s, [x2[l][i, 0] for i in range(2)])
-            y1[l][0, 1] = choose(x2_e, [x2[l][i, 1] for i in range(2)])
-            sends += [y1_copy(l, 0), y1_copy(l, 1)]
+            shifted(1, x2, l)
+            y1[l][0, 0] = choose(x2_s, [x2[l][k, 0] for k in range(2)])
+            y1[l][0, 1] = choose(x2_e, [x2[l][k, 1] for k in range(2)])
+            sends += [wide_copy(2, y1, l, way, (1, 15)) for way in range(2)]
         l = i - 9
         if 0 <= l < 4:
-            for way in range(2):
-                y1_copy(l, way).wait_recv()
-            y2[l][0, 0] = choose(y1_s, [y1[l][i, 0] for i in range(3)])
-            y2[l][0, 1] = choose(y1_e, [y1[l][i, 1] for i in range(3)])
-            sends += [y2_copy(l, 0), y2_copy(l, 1)]
+            shifted(2, y1, l)
+            y2[l][0, 0] = choose(y1_s, [y1[l][k, 0] for k in range(3)])
+            y2[l][0, 1] = choose(y1_e, [y1[l][k, 1] for k in range(3)])
+            sends += [half_copy(3, y2, l, half, (1, 15)) for half in range(2)]
         l = i - 11
         own = None
         if 0 <= l < 4:
-            for half in range(2):
-                y2_copy(l, half).wait_recv()
-            g_ref[0, 0, 4 + l, 0] = choose(y2_s, [y2[l][i, 0] for i in range(2)])
-            g_ref[0, 0, 4 + l, 1] = choose(y2_e, [y2[l][i, 1] for i in range(2)])
+            shifted(3, y2, l)
+            g_ref[0, 0, 4 + l, 0] = choose(y2_s, [y2[l][k, 0] for k in range(2)])
+            g_ref[0, 0, 4 + l, 1] = choose(y2_e, [y2[l][k, 1] for k in range(2)])
             own = 4 + l
-        if i > 0:
-            beside(i - 1)
+        beside(i - 1)
         for copy in sends:
             copy.start()
         if own is not None:
@@ -324,10 +329,10 @@
         ring(i)
 
     p_copy().wait()
+    last_ref[...] = probe_ref[:, pl.ds(pl.multiple_of(rem(z // 2 + 2, 4) * quad, HDIM), quad)]
     biggest(1)
     settle(0)
-    for q in range(4):
-        d_own(q).wait_recv()
+    own_beside(0)
 
     for by in range(1, 16):
         mx_copy(1, by).start()
@@ -345,37 +350,30 @@
             ring(slot)
         if slot == 21:
             settle(1)
-            for q in range(4, 8):
-                d_own(q).wait_recv()
+            own_beside(1)
         if slot in work:
             units(*work[slot])
 
-    for q in range(8):
-        d_own(q).wait_send()
-    for slot in range(28):
-        for way in range(2):
-            d, q = place(way, slot)
-            d_passed(way, slot, d, q).wait_send()
-            z_arrival(way, d, q, slot).wait_send()
-    for l in range(LAYERS):
-        a_copy(l).wait_send()
-        b_copy(l).wait_send()
-        for way in range(2):
-            x1_copy(l, way).wait_send()
-            x2_copy(l, way).wait_send()
-            y1_copy(l, way).wait_send()
-            y2_copy(l, way).wait_send()
-    for group in range(2):
-        for by in range(1, 16):
-            mx_copy(group, by).wait_send()
+    total(g_ref.at[pl.ds(0, 7), 0], z_send, z_recv.at[0]).wait_send()
+    total(g_ref.at[pl.ds(0, 8), 0], d_send, z_recv.at[0]).wait_send()
+    total(g_ref.at[pl.ds(0, 7), 0, pl.ds(0, 4)], xy_send, z_recv.at[0]).wait_send()
+    total(mx_ref.at[pl.ds(0, 2), pl.ds(1, 15)], mx_send, mx_recv.at[0]).wait_send()
+
+
+def piece(l, c):
+    if c < 2:
+        return 2 * (1 - c) + l // 2, l % 2
+    return 4 + l, c - 2
 
 
 def output_kernel(
-    src_ref, tgt_ref, c_ref, acc_ref, pk_ref,
+    src_ref, tgt_ref, c_ref, acc_ref, pk_ref, last_ref,
     codes_hbm, peaks_ref, checked_hbm,
     chk_ref, sem, chk_sem,
 ):
     col = lax.axis_index("col")
+    z = lax.axis_index("row") // 2
+    quad = c_ref.shape[2] // 4
     classes = recv_classes(src_ref, tgt_ref, col)
     slots = []
     for c in range(4):
@@ -391,26 +389,43 @@
     for l in range(LAYERS):
         for c in range(4):
             copy = pltpu.make_async_copy(
-                c_ref.at[c // 2 * 4 + l, c % 2], codes_hbm.at[l, :, lanes(c)], sem.at[l, c]
+                c_ref.at[piece(l, c)], codes_hbm.at[l, :, lanes(c)], sem.at[l, c]
             )
             copy.start()
             copies.append(copy)
-    for l in range(LAYERS):
-        for c in range(4):
-            half = c % 2
-            scale = pk_ref[c // 2, half * 4 + l:half * 4 + l + 1, :]
-            block = acc_ref[c // 2 * 4 + l, :, half * HDIM:(half + 1) * HDIM]
-            chk_ref[l, c] = (block * scale).astype(jnp.bfloat16)
-            copy = pltpu.make_async_copy(
-                chk_ref.at[l, c], checked_hbm.at[l, :, lanes(c)], chk_sem.at[l, c]
-            )
-            copy.start()
-            copies.append(copy)
+    start = pl.multiple_of(rem(z // 2 + 2, 4) * quad, HDIM)
+
+    def put(l, c, block):
+        q, half = piece(l, c)
+        scale = pk_ref[q // 4, half * 4 + q % 4:half * 4 + q % 4 + 1, :]
+        chk_ref[l, c] = (block * scale).astype(jnp.bfloat16)
+        copy = pltpu.make_async_copy(
+            chk_ref.at[l, c], checked_hbm.at[l, :, lanes(c)], chk_sem.at[l, c]
+        )
+        copy.start()
+        copies.append(copy)
+
+    for l in range(LAYERS):
+        for c in range(2):
+            q, half = piece(l, c)
+            put(l, c, acc_ref[q, :, half * HDIM:(half + 1) * HDIM])
+    for l in range(LAYERS):
+        both = jnp.concatenate(
+            [c_ref[4 + l, 0, pl.ds(start, quad), :], c_ref[4 + l, 1, pl.ds(start, quad), :]], axis=1
+        )
+        last = acc_ref[4 + l] + jnp.dot(
+            last_ref[...], both, preferred_element_type=jnp.float32
+        )
+        for c in range(2, 4):
+            put(l, c, last[:, (c - 2) * HDIM:(c - 1) * HDIM])
     lane = lax.broadcasted_iota(jnp.int32, (LAYERS, HDIM), 1)
     out = jnp.zeros((LAYERS, HDIM), jnp.float32)
     for c in range(4):
-        half = c % 2
-        out = jnp.where(lane == slots[c], pk_ref[c // 2, half * 4:half * 4 + 4, :], out)
+        rows = []
+        for l in range(LAYERS):
+            q, half = piece(l, c)
+            rows.append(pk_ref[q // 4, half * 4 + q % 4:half * 4 + q % 4 + 1, :])
+        out = jnp.where(lane == slots[c], jnp.concatenate(rows, axis=0), out)
     peaks_ref[...] = out[:, :PER]
     for copy in copies:
         copy.wait()
@@ -426,16 +441,17 @@
     three = pltpu.VMEM((3, 2, depth, HDIM), bf16)
     two = pltpu.VMEM((2, 2, depth, HDIM), bf16)
     dma = pltpu.SemaphoreType.DMA
-    c, acc, pk = pl.pallas_call(
+    c, acc, pk, held = pl.pallas_call(
         gather_kernel,
         name="gather_codes",
         out_shape=(
             pltpu.VMEM((8, 2, model, HDIM), bf16),
             pltpu.VMEM((8, tokens, 2 * HDIM), f32),
             pltpu.VMEM((2, 8, HDIM), f32),
+            pltpu.VMEM((tokens, model // 4), bf16),
         ),
         in_specs=[smem, smem, hbm, hbm],
-        out_specs=(vmem, vmem, vmem),
+        out_specs=(vmem, vmem, vmem, vmem),
         scratch_shapes=[
             pltpu.VMEM((NZ, 2, 8, 2, depth, HDIM), bf16),
             pltpu.VMEM((tokens, model), bf16),
@@ -447,12 +463,11 @@
         ]
         + [three] * 4 + [two] * 4 + [three] * 4 + [two] * 4
         + [
-            dma((4,)), dma, dma((4, 2)), dma((4, 2)), dma((4, 4, 2)), dma((4, 4, 2)),
-            dma((2, 28)), dma((2, 28)), dma((8,)), dma((8,)), dma((2, 28)), dma((2, 28)),
-            dma((2, 16)), dma((2, 16)),
+            dma((4,)), dma, dma((4, 2)), dma((4, 4)), dma((28,)), dma((2,)), dma((28,)), dma((2,)),
+            dma, dma, dma, dma,
         ],
         compiler_params=pltpu.CompilerParams(
-            collective_id=0, has_side_effects=True, vmem_limit_bytes=36 * 1024 * 1024
+            collective_id=0, has_side_effects=True, vmem_limit_bytes=34 * 1024 * 1024
         ),
     )(src_map, tgt_map, train_weight, probe)
     return pl.pallas_call(
@@ -463,15 +478,15 @@
             jax.ShapeDtypeStruct((layers, PER), f32),
             jax.ShapeDtypeStruct((layers, tokens, width), bf16),
         ),
-        in_specs=[smem, smem, vmem, vmem, vmem],
+        in_specs=[smem, smem, vmem, vmem, vmem, vmem],
         out_specs=(hbm, vmem, hbm),
         scratch_shapes=[
             pltpu.VMEM((layers, 4, tokens, HDIM), bf16),
             dma((4, 4)),
             dma((4, 4)),
         ],
-        compiler_params=pltpu.CompilerParams(vmem_limit_bytes=8 * 1024 * 1024),
-    )(src_map, tgt_map, c, acc, pk)
+        compiler_params=pltpu.CompilerParams(vmem_limit_bytes=4 * 1024 * 1024),
+    )(src_map, tgt_map, c, acc, pk, held)
 
 
 def solution(mesh):

time: 129 us -> 129 us (level)
  no operation moved by 1% of the time
where the time goes in v2:
time: 129 us
  Pallas kernels  128 us (99%)
    pallas_call x1, Pallas kernels, per_device(): pl.pallas_call(gather_kernel, name='gather_codes', out_shape=(pltpu.VMEM(...  119 us
    pallas_call x1, Pallas kernels, per_device(): pl.pallas_call(output_kernel, name='write_outputs', out_shape=(jax.ShapeD...  9.42 us

profile of v2, /device:TPU:1, one launch (start us, length us, event | category | flops | bytes accessed | tf_op | source)
XLA Modules:
  0.0 129.2 jit_solution(17744938578302520857)
XLA Ops:
  0.6 0.0 copy-start.1
  0.6 0.0 copy-start
  0.7 118.9 %gather_codes.1 = (bf16[8,2,4608,128]{3,2,1,0:T(8,128)(2,1)S(1)}, f32[8,512,256]{2,1,0:T(8,128)S(1)}, f32[2,8,128]{2,1,0:T(8,128)S(1)}, bf16[512,1152]{1,0:T(8,128)(2,1)S(1)}) custom-call(s32[64]{0:T(128)} %src_ref.3, s32[64]{0:T(128)} %tgt_ref.3, bf16[4,288,512]{2,1,0:T(8,128)(2,1)} %w_hbm.1, bf16[512,4608]{1,0:T(8,128)(2,1)} %probe_hbm.1), custom_call_target="tpu_custom_call" | custom-call | tf_op jit(solution)/shard_map/gather_codes/pallas_call | solution.py:444
  119.6 0.0 copy-done.1
  119.6 0.0 copy-done
  119.6 9.4 %write_outputs.1 = (bf16[4,4608,512]{2,1,0:T(8,128)(2,1)}, f32[4,4]{1,0:T(4,128)}, bf16[4,512,512]{2,1,0:T(8,128)(2,1)}) custom-call(s32[64]{0:T(128)S(1)} %copy-done, s32[64]{0:T(128)S(1)} %copy-done.1, bf16[8,2,4608,128]{3,2,1,0:T(8,128)(2,1)S(1)} %get-tuple-element.7.c_ref, f32[8,512,256]{2,1,0:T(8,128)S(1)} %get-tuple-element.8.acc_ref, ...), custom_call_target="tpu_custom_call" | custom-call | tf_op jit(solution)/shard_map/write_outputs/pallas_call | solution.py:473
Async XLA Ops:
  0.6 118.9 %copy-start.1 = (s32[64]{0:T(128)S(1)}, s32[64]{0:T(128)}, u32[]{:S(2)}) copy-start(s32[64]{0:T(128)} %tgt_ref.3) | copy-start | bytes 772
  0.6 118.9 %copy-start = (s32[64]{0:T(128)S(1)}, s32[64]{0:T(128)}, u32[]{:S(2)}) copy-start(s32[64]{0:T(128)} %src_ref.3) | copy-start | bytes 772

commit v3 on v2

--- a/solution.py
+++ b/solution.py
@@ -104,21 +104,27 @@
     barrier = pltpu.get_barrier_semaphore()
     for d in range(1, 16):
         pl.semaphore_signal(barrier, inc=1, device_id=(rem(row + d, 16), col), device_id_type=MESH)
-    for d in (8, 1, 15, 4, 12):
-        pl.semaphore_signal(barrier, inc=1, device_id=(row, rem(col + d, NCOL)), device_id_type=MESH)
+    y = rem(col, 4)
+    x_next, x_back = rem(col + 4, NCOL), rem(col + 12, NCOL)
+    y_next, y_back = col - y + rem(y + 1, 4), col - y + rem(y + 3, 4)
+    for to in (rem(col + 8, NCOL), rem(col + 1, NCOL), rem(col + 15, NCOL), x_next, x_back, y_next, y_back):
+        pl.semaphore_signal(barrier, inc=1, device_id=(row, to), device_id_type=MESH)
     for l in range(LAYERS):
         w_copy(l).start()
     p_copy().start()
 
     at_a, at_b, at_s, at_e, s_by, e_by = send_classes(src_ref, tgt_ref, col)
-    s_x, s_y = rem((s_by + 1) // 4, 4), rem(s_by + 1, 4) - 1
-    e_x, e_y = rem((e_by + 2) // 4, 4), rem(e_by + 2, 4) - 2
-    x1_s = jnp.where(s_x == 0, 0, jnp.where(s_x == 3, 2, 1))
-    x1_e = jnp.where(e_x == 0, 0, jnp.where(e_x == 1, 1, 2))
-    x2_s, x2_e = jnp.where(s_x == 2, 1, 0), jnp.where(e_x == 2, 1, 0)
-    y1_s = jnp.where(s_y == 0, 0, jnp.where(s_y == -1, 2, 1))
-    y1_e = jnp.where(e_y == 0, 0, jnp.where(e_y == 1, 1, 2))
-    y2_s, y2_e = jnp.where(s_y == 2, 1, 0), jnp.where(e_y == -2, 1, 0)
+    s_y, e_y = rem(s_by, 4), rem(e_by, 4)
+    s_x = rem(s_by // 4 + jnp.where(y < s_y, 1, 0), 4)
+    e_x = rem(e_by // 4 + jnp.where(y < e_y, 1, 0), 4)
+
+    def steps(s_part, e_part):
+        first_s = jnp.where(s_part == 0, 0, jnp.where(s_part == 3, 2, 1))
+        first_e = jnp.where(e_part == 0, 0, jnp.where(e_part == 1, 1, 2))
+        return first_s, first_e, jnp.where(s_part == 2, 1, 0), jnp.where(e_part == 2, 1, 0)
+
+    y1_s, y1_e, y2_s, y2_e = steps(s_y, e_y)
+    x1_s, x1_e, x2_s, x2_e = steps(s_x, e_x)
 
     def choose(at, values):
         out = values[-1]
@@ -133,14 +139,14 @@
         w_copy(l).wait()
         sb_ref[l, 0] = head(l, at_a)
         sb_ref[l, 1] = head(l, at_b)
-        x1[l][0, 0] = head(l, at_s)
-        x1[l][0, 1] = head(l, at_e)
+        y1[l][0, 0] = head(l, at_s)
+        y1[l][0, 1] = head(l, at_e)
 
     @pl.loop(0, 8)
     def _(q):
         acc_ref[q] = jnp.zeros(acc_ref.shape[1:], jnp.float32)
 
-    pl.semaphore_wait(barrier, 20)
+    pl.semaphore_wait(barrier, 22)
 
     def total(part, send, recv):
         return pltpu.make_async_remote_copy(
@@ -148,23 +154,23 @@
             device_id=(row, rem(col + 1, NCOL)), device_id_type=MESH,
         )
 
-    def to_col(src, dst, recv, by):
+    def to_col(src, dst, recv, to):
         return pltpu.make_async_remote_copy(
             src_ref=src, dst_ref=dst, send_sem=xy_send, recv_sem=recv,
-            device_id=(row, rem(col + by, NCOL)), device_id_type=MESH,
+            device_id=(row, to), device_id_type=MESH,
         )
 
     def a_copy(l):
-        return to_col(sb_ref.at[l, 0], g_ref.at[0, 0, 2 + l // 2, l % 2], ab_recv.at[l, 0], 8)
+        return to_col(sb_ref.at[l, 0], g_ref.at[0, 0, 2 + l // 2, l % 2], ab_recv.at[l, 0], rem(col + 8, NCOL))
 
     def b_copy(l):
-        return to_col(sb_ref.at[l, 1], g_ref.at[0, 0, l // 2, l % 2], ab_recv.at[l, 1], 1)
-
-    def wide_copy(stage, buffer, l, way, by):
-        return to_col(buffer[l].at[0], buffer[l].at[1 + way], xy_recv.at[stage, l], by[way])
-
-    def half_copy(stage, buffer, l, half, by):
-        return to_col(buffer[l].at[0, half], buffer[l].at[1, half], xy_recv.at[stage, l], by[half])
+        return to_col(sb_ref.at[l, 1], g_ref.at[0, 0, l // 2, l % 2], ab_recv.at[l, 1], rem(col + 1, NCOL))
+
+    def wide_copy(stage, buffer, l, way, to):
+        return to_col(buffer[l].at[0], buffer[l].at[1 + way], xy_recv.at[stage, l], to[way])
+
+    def half_copy(stage, buffer, l, half, to):
+        return to_col(buffer[l].at[0, half], buffer[l].at[1, half], xy_recv.at[stage, l], to[half])
 
     def shifted(stage, buffer, l):
         part = buffer[l].at[pl.ds(0, 2)] if stage % 2 == 0 else buffer[l].at[0]
@@ -175,7 +181,7 @@
         a_copy(l).start()
     for l in range(LAYERS):
         for way in range(2):
-            wide_copy(0, x1, l, way, (4, 12)).start()
+            wide_copy(0, y1, l, way, (y_next, y_back)).start()
 
     def z_copy(way, d, at, slot):
         to = rem(z + (1, NZ - 1)[way], NZ) * 2 + core
@@ -295,31 +301,31 @@
         if i == 3:
             for by in range(1, 16):
                 mx_copy(0, by).start()
+        sends = []
         l = i - 4
-        sends = []
         if 0 <= l < 4:
-            shifted(0, x1, l)
+            shifted(0, y1, l)
+            y2[l][0, 0] = choose(y1_s, [y1[l][k, 0] for k in range(3)])
+            y2[l][0, 1] = choose(y1_e, [y1[l][k, 1] for k in range(3)])
+            sends += [half_copy(1, y2, l, half, (y_next, y_back)) for half in range(2)]
+        l = i - 7
+        if 0 <= l < 4:
+            shifted(1, y2, l)
+            x1[l][0, 0] = choose(y2_s, [y2[l][k, 0] for k in range(2)])
+            x1[l][0, 1] = choose(y2_e, [y2[l][k, 1] for k in range(2)])
+            sends += [wide_copy(2, x1, l, way, (x_next, x_back)) for way in range(2)]
+        l = i - 9
+        if 0 <= l < 4:
+            shifted(2, x1, l)
             x2[l][0, 0] = choose(x1_s, [x1[l][k, 0] for k in range(3)])
             x2[l][0, 1] = choose(x1_e, [x1[l][k, 1] for k in range(3)])
-            sends += [half_copy(1, x2, l, half, (4, 12)) for half in range(2)]
-        l = i - 7
-        if 0 <= l < 4:
-            shifted(1, x2, l)
-            y1[l][0, 0] = choose(x2_s, [x2[l][k, 0] for k in range(2)])
-            y1[l][0, 1] = choose(x2_e, [x2[l][k, 1] for k in range(2)])
-            sends += [wide_copy(2, y1, l, way, (1, 15)) for way in range(2)]
-        l = i - 9
-        if 0 <= l < 4:
-            shifted(2, y1, l)
-            y2[l][0, 0] = choose(y1_s, [y1[l][k, 0] for k in range(3)])
-            y2[l][0, 1] = choose(y1_e, [y1[l][k, 1] for k in range(3)])
-            sends += [half_copy(3, y2, l, half, (1, 15)) for half in range(2)]
+            sends += [half_copy(3, x2, l, half, (x_next, x_back)) for half in range(2)]
         l = i - 11
         own = None
         if 0 <= l < 4:
-            shifted(3, y2, l)
-            g_ref[0, 0, 4 + l, 0] = choose(y2_s, [y2[l][k, 0] for k in range(2)])
-            g_ref[0, 0, 4 + l, 1] = choose(y2_e, [y2[l][k, 1] for k in range(2)])
+            shifted(3, x2, l)
+            g_ref[0, 0, 4 + l, 0] = choose(x2_s, [x2[l][k, 0] for k in range(2)])
+            g_ref[0, 0, 4 + l, 1] = choose(x2_e, [x2[l][k, 1] for k in range(2)])
             own = 4 + l
         beside(i - 1)
         for copy in sends:

time: 129 us -> 126 us (0.977)
  Pallas kernels: 128 us -> 125 us
    pallas_call x1, Pallas kernels: 119 us -> 116 us  [per_device(): pl.pallas_call(gather_kernel, name='gather_codes', out_shape=(pltpu.VMEM(...]
where the time goes in v3:
time: 126 us
  Pallas kernels  125 us (99%)
    pallas_call x1, Pallas kernels, per_device(): pl.pallas_call(gather_kernel, name='gather_codes', out_shape=(pltpu.VMEM(...  116 us
    pallas_call x1, Pallas kernels, per_device(): pl.pallas_call(output_kernel, name='write_outputs', out_shape=(jax.ShapeD...  9.42 us

profile of v3, /device:TPU:1, one launch (start us, length us, event | category | flops | bytes accessed | tf_op | source)
XLA Modules:
  0.0 126.3 jit_solution(8724040710116640595)
XLA Ops:
  0.6 0.0 copy-start.1
  0.6 0.0 copy-start
  0.7 116.0 %gather_codes.1 = (bf16[8,2,4608,128]{3,2,1,0:T(8,128)(2,1)S(1)}, f32[8,512,256]{2,1,0:T(8,128)S(1)}, f32[2,8,128]{2,1,0:T(8,128)S(1)}, bf16[512,1152]{1,0:T(8,128)(2,1)S(1)}) custom-call(s32[64]{0:T(128)} %src_ref.3, s32[64]{0:T(128)} %tgt_ref.3, bf16[4,288,512]{2,1,0:T(8,128)(2,1)} %w_hbm.1, bf16[512,4608]{1,0:T(8,128)(2,1)} %probe_hbm.1), custom_call_target="tpu_custom_call" | custom-call | tf_op jit(solution)/shard_map/gather_codes/pallas_call | solution.py:450
  116.7 0.0 copy-done.1
  116.7 0.0 copy-done
  116.7 9.4 %write_outputs.1 = (bf16[4,4608,512]{2,1,0:T(8,128)(2,1)}, f32[4,4]{1,0:T(4,128)}, bf16[4,512,512]{2,1,0:T(8,128)(2,1)}) custom-call(s32[64]{0:T(128)S(1)} %copy-done, s32[64]{0:T(128)S(1)} %copy-done.1, bf16[8,2,4608,128]{3,2,1,0:T(8,128)(2,1)S(1)} %get-tuple-element.7.c_ref, f32[8,512,256]{2,1,0:T(8,128)S(1)} %get-tuple-element.8.acc_ref, ...), custom_call_target="tpu_custom_call" | custom-call | tf_op jit(solution)/shard_map/write_outputs/pallas_call | solution.py:479
Async XLA Ops:
  0.6 116.1 %copy-start.1 = (s32[64]{0:T(128)S(1)}, s32[64]{0:T(128)}, u32[]{:S(2)}) copy-start(s32[64]{0:T(128)} %tgt_ref.3) | copy-start | bytes 772
  0.6 116.1 %copy-start = (s32[64]{0:T(128)S(1)}, s32[64]{0:T(128)}, u32[]{:S(2)}) copy-start(s32[64]{0:T(128)} %src_ref.3) | copy-start | bytes 772

commit v4 on v3

--- a/solution.py
+++ b/solution.py
@@ -139,12 +139,6 @@
         w_copy(l).wait()
         sb_ref[l, 0] = head(l, at_a)
         sb_ref[l, 1] = head(l, at_b)
-        y1[l][0, 0] = head(l, at_s)
-        y1[l][0, 1] = head(l, at_e)
-
-    @pl.loop(0, 8)
-    def _(q):
-        acc_ref[q] = jnp.zeros(acc_ref.shape[1:], jnp.float32)
 
     pl.semaphore_wait(barrier, 22)
 
@@ -180,8 +174,8 @@
         b_copy(l).start()
         a_copy(l).start()
     for l in range(LAYERS):
-        for way in range(2):
-            wide_copy(0, y1, l, way, (y_next, y_back)).start()
+        y1[l][0, 0] = head(l, at_s)
+        y1[l][0, 1] = head(l, at_e)
 
     def z_copy(way, d, at, slot):
         to = rem(z + (1, NZ - 1)[way], NZ) * 2 + core
@@ -284,7 +278,14 @@
         (a_copy, b_copy)[kind](l).wait_recv()
         send_own(2 * (1 - kind) + l // 2, l % 2)
 
+    @pl.loop(0, 8)
+    def _(q):
+        acc_ref[q] = jnp.zeros(acc_ref.shape[1:], jnp.float32)
+
     took(1, 0)
+    for l in range(LAYERS):
+        for way in range(2):
+            wide_copy(0, y1, l, way, (y_next, y_back)).start()
     took(1, 1)
     took(0, 0)
     took(1, 2)

time: 126 us -> 126 us (level)
  no operation moved by 1% of the time
where the time goes in v4:
time: 126 us
  Pallas kernels  125 us (99%)
    pallas_call x1, Pallas kernels, per_device(): pl.pallas_call(gather_kernel, name='gather_codes', out_shape=(pltpu.VMEM(...  116 us
    pallas_call x1, Pallas kernels, per_device(): pl.pallas_call(output_kernel, name='write_outputs', out_shape=(jax.ShapeD...  9.42 us

profile of v4, /device:TPU:1, one launch (start us, length us, event | category | flops | bytes accessed | tf_op | source)
XLA Modules:
  0.0 126.3 jit_solution(13726350416884488055)
XLA Ops:
  0.6 0.0 copy-start.1
  0.6 0.0 copy-start
  0.7 116.1 %gather_codes.1 = (bf16[8,2,4608,128]{3,2,1,0:T(8,128)(2,1)S(1)}, f32[8,512,256]{2,1,0:T(8,128)S(1)}, f32[2,8,128]{2,1,0:T(8,128)S(1)}, bf16[512,1152]{1,0:T(8,128)(2,1)S(1)}) custom-call(s32[64]{0:T(128)} %src_ref.3, s32[64]{0:T(128)} %tgt_ref.3, bf16[4,288,512]{2,1,0:T(8,128)(2,1)} %w_hbm.1, bf16[512,4608]{1,0:T(8,128)(2,1)} %probe_hbm.1), custom_call_target="tpu_custom_call" | custom-call | tf_op jit(solution)/shard_map/gather_codes/pallas_call | solution.py:451
  116.7 0.0 copy-done.1
  116.7 0.0 copy-done
  116.7 9.4 %write_outputs.1 = (bf16[4,4608,512]{2,1,0:T(8,128)(2,1)}, f32[4,4]{1,0:T(4,128)}, bf16[4,512,512]{2,1,0:T(8,128)(2,1)}) custom-call(s32[64]{0:T(128)S(1)} %copy-done, s32[64]{0:T(128)S(1)} %copy-done.1, bf16[8,2,4608,128]{3,2,1,0:T(8,128)(2,1)S(1)} %get-tuple-element.7.c_ref, f32[8,512,256]{2,1,0:T(8,128)S(1)} %get-tuple-element.8.acc_ref, ...), custom_call_target="tpu_custom_call" | custom-call | tf_op jit(solution)/shard_map/write_outputs/pallas_call | solution.py:480
Async XLA Ops:
  0.6 116.1 %copy-start.1 = (s32[64]{0:T(128)S(1)}, s32[64]{0:T(128)}, u32[]{:S(2)}) copy-start(s32[64]{0:T(128)} %tgt_ref.3) | copy-start | bytes 772
  0.6 116.1 %copy-start = (s32[64]{0:T(128)S(1)}, s32[64]{0:T(128)}, u32[]{:S(2)}) copy-start(s32[64]{0:T(128)} %src_ref.3) | copy-start | bytes 772

commit v5 on v3

--- a/solution.py
+++ b/solution.py
@@ -166,6 +166,15 @@
     def b_copy(l):
         return to_col(sb_ref.at[l, 1], g_ref.at[0, 0, l // 2, l % 2], ab_recv.at[l, 1], rem(col + 1, NCOL))
 
+    def first_rows(part):
+        return pl.ds(part * (depth // 2), depth // 2)
+
+    def first_copy(part):
+        rows = first_rows(part)
+        return to_col(
+            sb_ref.at[0, 1, rows], g_ref.at[0, 0, 0, 0, rows], ab_recv.at[4 * part, 1], rem(col + 1, NCOL)
+        )
+
     def wide_copy(stage, buffer, l, way, to):
         return to_col(buffer[l].at[0], buffer[l].at[1 + way], xy_recv.at[stage, l], to[way])
 
@@ -177,7 +186,11 @@
         total(part, xy_send, xy_recv.at[stage, l]).wait_recv()
 
     for l in range(LAYERS):
-        b_copy(l).start()
+        if l == 0:
+            for part in range(2):
+                first_copy(part).start()
+        else:
+            b_copy(l).start()
         a_copy(l).start()
     for l in range(LAYERS):
         for way in range(2):
@@ -271,7 +284,7 @@
                     c_ref[q, half, pl.ds(pl.multiple_of(at, 16), depth), :] = (
                         (block.astype(jnp.float32) * 0.0625) * scale
                     ).astype(jnp.bfloat16)
-        if group == 1 and t == 3:
+        if group == 1 and t == 3 and l >= 2:
             return
         both = jnp.concatenate(
             [c_ref[q, 0, pl.ds(start, quad), :], c_ref[q, 1, pl.ds(start, quad), :]], axis=1
@@ -284,7 +297,10 @@
         (a_copy, b_copy)[kind](l).wait_recv()
         send_own(2 * (1 - kind) + l // 2, l % 2)
 
-    took(1, 0)
+    for part in range(2):
+        first_copy(part).wait_recv()
+        for way in range(2):
+            z_copy(way, 0, (0, 0, first_rows(part)), 0).start()
     took(1, 1)
     took(0, 0)
     took(1, 2)
@@ -416,12 +432,12 @@
             q, half = piece(l, c)
             put(l, c, acc_ref[q, :, half * HDIM:(half + 1) * HDIM])
     for l in range(LAYERS):
-        both = jnp.concatenate(
-            [c_ref[4 + l, 0, pl.ds(start, quad), :], c_ref[4 + l, 1, pl.ds(start, quad), :]], axis=1
-        )
-        last = acc_ref[4 + l] + jnp.dot(
-            last_ref[...], both, preferred_element_type=jnp.float32
-        )
+        last = acc_ref[4 + l]
+        if l >= 2:
+            both = jnp.concatenate(
+                [c_ref[4 + l, 0, pl.ds(start, quad), :], c_ref[4 + l, 1, pl.ds(start, quad), :]], axis=1
+            )
+            last = last + jnp.dot(last_ref[...], both, preferred_element_type=jnp.float32)
         for c in range(2, 4):
             put(l, c, last[:, (c - 2) * HDIM:(c - 1) * HDIM])
     lane = lax.broadcasted_iota(jnp.int32, (LAYERS, HDIM), 1)
@@ -469,7 +485,7 @@
         ]
         + [three] * 4 + [two] * 4 + [three] * 4 + [two] * 4
         + [
-            dma((4,)), dma, dma((4, 2)), dma((4, 4)), dma((28,)), dma((2,)), dma((28,)), dma((2,)),
+            dma((4,)), dma, dma((5, 2)), dma((4, 4)), dma((28,)), dma((2,)), dma((28,)), dma((2,)),
             dma, dma, dma, dma,
         ],
         compiler_params=pltpu.CompilerParams(

time: 126 us -> 126 us (level)
  no operation moved by 1% of the time
where the time goes in v5:
time: 126 us
  Pallas kernels  125 us (99%)
    pallas_call x1, Pallas kernels, per_device(): pl.pallas_call(gather_kernel, name='gather_codes', out_shape=(pltpu.VMEM(...  116 us
    pallas_call x1, Pallas kernels, per_device(): pl.pallas_call(output_kernel, name='write_outputs', out_shape=(jax.ShapeD...  9.39 us

profile of v5, /device:TPU:1, one launch (start us, length us, event | category | flops | bytes accessed | tf_op | source)
XLA Modules:
  0.0 126.3 jit_solution(2748669373034935484)
XLA Ops:
  0.6 0.0 copy-start.1
  0.6 0.0 copy-start
  0.7 116.0 %gather_codes.1 = (bf16[8,2,4608,128]{3,2,1,0:T(8,128)(2,1)S(1)}, f32[8,512,256]{2,1,0:T(8,128)S(1)}, f32[2,8,128]{2,1,0:T(8,128)S(1)}, bf16[512,1152]{1,0:T(8,128)(2,1)S(1)}) custom-call(s32[64]{0:T(128)} %src_ref.3, s32[64]{0:T(128)} %tgt_ref.3, bf16[4,288,512]{2,1,0:T(8,128)(2,1)} %w_hbm.1, bf16[512,4608]{1,0:T(8,128)(2,1)} %probe_hbm.1), custom_call_target="tpu_custom_call" | custom-call | tf_op jit(solution)/shard_map/gather_codes/pallas_call | solution.py:466
  116.7 0.0 copy-done.1
  116.7 0.0 copy-done
  116.7 9.4 %write_outputs.1 = (bf16[4,4608,512]{2,1,0:T(8,128)(2,1)}, f32[4,4]{1,0:T(4,128)}, bf16[4,512,512]{2,1,0:T(8,128)(2,1)}) custom-call(s32[64]{0:T(128)S(1)} %copy-done, s32[64]{0:T(128)S(1)} %copy-done.1, bf16[8,2,4608,128]{3,2,1,0:T(8,128)(2,1)S(1)} %get-tuple-element.7.c_ref, f32[8,512,256]{2,1,0:T(8,128)S(1)} %get-tuple-element.8.acc_ref, ...), custom_call_target="tpu_custom_call" | custom-call | tf_op jit(solution)/shard_map/write_outputs/pallas_call | solution.py:495
Async XLA Ops:
  0.6 116.1 %copy-start.1 = (s32[64]{0:T(128)S(1)}, s32[64]{0:T(128)}, u32[]{:S(2)}) copy-start(s32[64]{0:T(128)} %tgt_ref.3) | copy-start | bytes 772
  0.6 116.1 %copy-start = (s32[64]{0:T(128)S(1)}, s32[64]{0:T(128)}, u32[]{:S(2)}) copy-start(s32[64]{0:T(128)} %src_ref.3) | copy-start | bytes 772
